TPU v7x, 32 devices: a 4x4x1 block of a 4x4x8 slice. The times are simulated.
32 devices in a mesh: dp: 1 (over z), tp: 4 (over y), sp: 8 (over x, core).
Axes of the slice: x: 4, y: 4, z: 1, core: 2. Of those that a mesh axis runs over, the one named last changes fastest.
The devices are a block of a 4x4x8 slice.
Arguments:
- hidden: bfloat16 [256, 4096], P('dp')
- ln_gain: bfloat16 [4096], replicated
- ln_bias: bfloat16 [4096], replicated
- w_q: bfloat16 [4096, 4096], P(None, 'tp')
- w_k: bfloat16 [4096, 1024], P(None, 'tp')
- w_v: bfloat16 [4096, 1024], P(None, 'tp')
- w_o: bfloat16 [4096, 4096], P('tp')
- k_cache: bfloat16 [256, 1024, 8, 128], P('dp', 'sp', 'tp')
- v_cache: bfloat16 [256, 1024, 8, 128], P('dp', 'sp', 'tp')
- lengths: int32 [256], P('dp')
Outputs:
- output 1: bfloat16 [256, 4096], P('dp')
- output 2: bfloat16 [256, 8, 128], P('dp', 'tp')
- output 3: bfloat16 [256, 8, 128], P('dp', 'tp')
All inputs are finite; a program needn't handle non-finite values.
Results may differ from a plain program's by a relative error of at most 0.0043512.
Values sent between devices are 32-bit elements.
A program may use at most 768 MiB of HBM per device.

v0:
```python
import jax
import jax.numpy as jnp
from jax import lax
from jax.sharding import PartitionSpec as P, NamedSharding


def norm_one_plus(hidden, ln_gain, ln_bias):
    wide = hidden.astype(jnp.float32)
    row_mean = jnp.mean(wide, axis=-1, keepdims=True)
    centred = wide - row_mean
    row_var = jnp.mean(centred * centred, axis=-1, keepdims=True)
    scaled = centred * lax.rsqrt(row_var + 1e-5)
    return (scaled * (1.0 + ln_gain.astype(jnp.float32)) + ln_bias.astype(jnp.float32)).astype(jnp.bfloat16)


def rotate_first(head_vecs, rot_pos, rot_dim):
    half_rot = rot_dim // 2
    inv_freq = 10000.0 ** (-2.0 * jnp.arange(half_rot, dtype=jnp.float32) / rot_dim)
    rot_angle = rot_pos.astype(jnp.float32)[..., None] * inv_freq
    cos_part = jnp.cos(rot_angle)
    sin_part = jnp.sin(rot_angle)
    lead_part = head_vecs[..., :half_rot]
    tail_part = head_vecs[..., half_rot:rot_dim]
    return jnp.concatenate([lead_part * cos_part - tail_part * sin_part, tail_part * cos_part + lead_part * sin_part, head_vecs[..., rot_dim:]], axis=-1)


def solution(mesh):
    def local_step(hidden, ln_gain, ln_bias, w_q, w_k, w_v, w_o, k_cache, v_cache, lengths):
        batch_rows, seq_local, kv_local, head_dim = k_cache.shape
        group_size = w_q.shape[1] // (head_dim * kv_local)
        rot_dim = head_dim // 2
        score_scale = head_dim ** -0.5
        normed = norm_one_plus(hidden, ln_gain, ln_bias)
        q_proj = jnp.dot(normed, w_q, preferred_element_type=jnp.float32).reshape(batch_rows, kv_local, group_size, head_dim)
        queries = rotate_first(q_proj, lengths[:, None, None], rot_dim).astype(jnp.bfloat16)
        k_proj = jnp.dot(normed, w_k, preferred_element_type=jnp.float32).reshape(batch_rows, kv_local, head_dim)
        k_new = rotate_first(k_proj, lengths[:, None], rot_dim).astype(jnp.bfloat16)
        v_new = jnp.dot(normed, w_v, preferred_element_type=jnp.float32).astype(jnp.bfloat16).reshape(batch_rows, kv_local, head_dim)
        block_index = lax.axis_index('sp')
        positions = block_index * seq_local + jnp.arange(seq_local)
        valid = positions[None, :] < lengths[:, None]
        scores = jnp.einsum('bkgd,bskd->bkgs', queries, k_cache, preferred_element_type=jnp.float32) * score_scale
        scores = jnp.where(valid[:, None, None, :], scores, -jnp.inf)
        owner = (lengths // seq_local) == block_index
        self_score = jnp.einsum('clhe,cle->clh', queries, k_new, preferred_element_type=jnp.float32) * score_scale
        self_score = jnp.where(owner[:, None, None], self_score, -jnp.inf)
        block_max = jnp.maximum(jnp.max(scores, axis=-1), self_score)
        safe_max = jnp.where(jnp.isfinite(block_max), block_max, 0.0)
        weights = jnp.exp(scores - safe_max[..., None])
        self_weight = jnp.exp(self_score - safe_max)
        weight_sum = jnp.sum(weights, axis=-1) + self_weight
        weighted = jnp.einsum('bkgs,bskd->bkgd', weights.astype(jnp.bfloat16), v_cache, preferred_element_type=jnp.float32)
        weighted = weighted + self_weight[..., None] * v_new.astype(jnp.float32)[:, :, None, :]
        packed = jnp.concatenate([weighted, block_max[..., None], weight_sum[..., None]], axis=-1)
        gathered = lax.all_gather(packed, 'sp', axis=0)
        all_max = gathered[..., head_dim]
        global_max = jnp.max(all_max, axis=0)
        factor = jnp.exp(all_max - global_max)
        total = jnp.sum(gathered[..., head_dim + 1] * factor, axis=0)
        context = jnp.sum(gathered[..., :head_dim] * factor[..., None], axis=0) / total[..., None]
        context = context.astype(jnp.bfloat16).reshape(batch_rows, kv_local * group_size * head_dim)
        partial_out = jnp.dot(context, w_o, preferred_element_type=jnp.float32)
        summed = lax.psum(partial_out, 'tp')
        out = (hidden.astype(jnp.float32) + summed).astype(jnp.bfloat16)
        return out, k_new, v_new

    row_spec = P('dp', None)
    cache_spec = P('dp', 'sp', 'tp', None)
    head_spec = P('dp', 'tp', None)
    return jax.shard_map(local_step, mesh=mesh, in_specs=(row_spec, P(None), P(None), P(None, 'tp'), P(None, 'tp'), P(None, 'tp'), P('tp', None), cache_spec, cache_spec, P('dp')), out_specs=(row_spec, head_spec, head_spec), check_vma=False)
```

profile of v0, /device:TPU:97, one launch (start us, length us, event | category | flops | bytes accessed | tf_op | source)
XLA Modules:
  0.0 254.2 jit_solution(12449723709595862698)
XLA Ops:
  7.2 0.0 copy-start
  7.2 0.0 copy-start.10
  7.2 0.0 copy-start.11
  7.2 0.1 all-gather.3.cloned.1.call-start
  7.3 0.0 copy-start.2
  7.3 2.1 convert_reduce_fusion
  9.4 2.3 fusion.7
  11.7 0.0 copy-done.10
  11.7 0.0 copy-done.11
  11.8 0.0 copy-done.2
  11.8 0.0 copy-start.9
  11.8 1.0 fusion.10
  12.8 0.0 copy-start.3
  12.8 1.3 copy-done.3
  14.2 0.0 copy-done
  14.2 1.0 fusion.36
  15.1 0.0 copy-start.4
  15.2 0.6 fusion.33
  15.8 0.0 copy-done.9
  15.8 0.7 broadcast_compare_fusion
  16.6 3.1 %convolution_convert_fusion = bf16[256,256]{0,1:T(8,128)(2,1)S(1)} fusion(bf16[256,4096]{1,0:T(8,128)(2,1)} %copy-done.3, bf16[4096,256]{1,0:T(8,128)(2,1)} %param.15), kind=kOutput, calls=%fused_computation.19 | convolution fusion | flops 536936448 | bytes 4325376 | tf_op jit(solution)/shard_map/dot_general | solution.py:38
  19.7 0.1 copy.108
  19.8 0.8 copy.109
  20.7 0.0 copy-done.4
  20.7 5.7 %fusion.35 = f32[256,1024]{1,0:T(8,128)S(1)} fusion(bf16[256,4096]{1,0:T(8,128)(2,1)S(1)} %copy-done.4, bf16[4096,1024]{1,0:T(8,128)(2,1)} %param.13), kind=kOutput, calls=%fused_computation.64 | convolution fusion | flops 2147483648 | bytes 11534336 | tf_op jit(solution)/shard_map/dot_general | solution.py:34
  26.4 0.5 reshape.193
  26.9 0.1 copy.130
  27.0 1.0 copy.129
  28.0 0.1 copy.128
  28.2 0.3 slice.60
  28.5 0.5 multiply_cosine_fusion
  29.0 0.0 copy-start.8
  29.0 0.9 subtract_convert_fusion
  29.9 0.3 subtract_convert_fusion.1
  30.2 0.0 copy-start.6
  30.2 0.6 fusion.48
  30.8 1.2 pad_maximum_fusion.1
  32.0 0.7 fusion.25
  32.7 12.8 %fusion.34 = (f32[256,2,4]{2,1,0:T(2,128)S(1)}, f32[256,2,4,128]{3,2,1,0:T(4,128)S(1)}) fusion(bf16[256,2,4,128]{3,2,1,0:T(4,128)(2,1)S(1)} %pad_maximum_fusion.1, bf16[256,128,2,128]{3,2,1,0:T(2,128)(2,1)} %param.17, pred[256,128]{1,0:T(8,128)(4,1)S(1)} %copy-done.8), kind=kOutput, calls=%fused_computation.63 | convolution fusion | flops 67893248 | bytes 18391040 | tf_op jit(solution)/shard_map/bkgd,bskd->bkgs/dot_general | solution.py:42
  45.4 0.3 is-finite_select_fusion
  45.8 1.4 fusion.21
  47.2 1.7 add_bitcast_fusion
  48.9 3.2 %copy.113 = f32[256,2,4,1]{3,2,1,0:T(4,128)S(1)} copy(f32[256,2,4,1]{2,1,0,3:T(2,128)S(1)} %get-tuple-element.27) | data formatting | bytes 16384 | tf_op jit(solution)/shard_map/broadcast_in_dim | solution.py:54
  52.1 4.1 %copy.112 = f32[256,2,4,1]{3,2,1,0:T(4,128)} copy(f32[256,2,4,1]{2,1,0,3:T(2,128)S(1)} %get-tuple-element.33) | data formatting | bytes 16384 | tf_op jit(solution)/shard_map/broadcast_in_dim | solution.py:54
  56.2 11.7 %fusion.15 = f32[256,2,4,128]{3,2,1,0:T(4,128)S(1)} fusion(bf16[256,128,2,128]{3,2,1,0:T(2,128)(2,1)} %param.18, f32[256,2,4,128]{3,2,1,0:T(4,128)S(1)} %get-tuple-element.39, f32[256,2,128]{2,1,0:T(2,128)} %copy.109, f32[256,2,4]{2,1,0:T(2,128)} %get-tuple-element.28, f32[256,2,4]{2,1,0:T(2,128)S(1)} %is-finite_select_fusion), kind=kOutput, calls=%fused_computation.18 | convolution fusion | flops 68157440 | bytes 19152896 | tf_op jit(solution)/shard_map/bkgs,bskd->bkgd/dot_general | solution.py:52
  67.9 0.8 pad_maximum_fusion
  68.7 2.2 copy.114
  70.9 0.1 all-gather.3.cloned.1.call-update
  70.9 0.1 all-reduce.2.cloned.1.call-start
  71.0 55.3 %all-gather.3.cloned.1.call-done = f32[2048,2,4,130]{0,2,3,1:T(4,128)} async-done(((f32[256,2,4,130]{0,2,3,1:T(4,128)}), f32[2048,2,4,130]{0,2,3,1:T(4,128)}) %all-gather.3.cloned.1.call-update) | async-done | bytes 8519696 | tf_op jit(solution)/shard_map/all_gather | solution.py:55
  126.3 10.9 %reshape.199 = f32[8,256,2,4,130]{1,0,3,4,2:T(8,128)} reshape(f32[2048,2,4,130]{0,2,3,1:T(4,128)} %all-gather.3.cloned.1.call-done) | data formatting | bytes 17039360 | tf_op jit(solution)/shard_map/all_gather | solution.py:55
  137.2 0.9 bitcast_reduce_fusion
  138.1 0.9 fusion.28
  139.0 0.9 fusion.31
  139.8 6.7 %fusion.4 = f32[256,2,4,128]{0,2,1,3:T(4,128)S(1)} fusion(f32[8,256,2,4]{1,0,3,2:T(8,128)S(1)} %fusion.31, f32[8,256,2,4,130]{1,0,3,4,2:T(8,128)} %reshape.199), kind=kLoop, calls=%fused_computation.5 | loop fusion | flops 3932160 | bytes 9502720 | tf_op jit(solution)/shard_map/reduce_sum | solution.py:60
  146.5 0.2 divide_convert_fusion
  146.7 0.1 copy.116
  146.9 7.7 %fusion.37 = f32[256,4096]{1,0:T(8,128)} fusion(bf16[256,1024]{0,1:T(8,128)(2,1)S(1)} %bitcast.47, bf16[1024,4096]{1,0:T(8,128)(2,1)} %param.16), kind=kOutput, calls=%fused_computation.66 | convolution fusion | flops 2147483648 | bytes 13107200 | tf_op jit(solution)/shard_map/dot_general | solution.py:62
  154.6 0.1 all-reduce.2.cloned.1.call-update
  154.6 0.8 copy.117
  155.4 0.1 copy-done.7
  155.5 1.2 pad_maximum_fusion.2
  156.7 85.9 %all-reduce.2.cloned.1.call-done = f32[256,4096]{1,0:T(8,128)} async-done(((f32[256,4096]{1,0:T(8,128)}), f32[256,4096]{1,0:T(8,128)}) %all-reduce.2.cloned.1.call-update) | async-done | bytes 4194320 | tf_op jit(solution)/shard_map/psum | solution.py:63
  242.6 4.7 %fusion.11 = bf16[256,4096]{1,0:T(8,128)(2,1)} fusion(f32[256,4096]{1,0:T(8,128)} %all-reduce.2.cloned.1.call-done, bf16[256,4096]{1,0:T(8,128)(2,1)} %param.10), kind=kLoop, calls=%fused_computation.15 | loop fusion | flops 3145728 | bytes 8388608 | tf_op jit(solution)/shard_map/convert_element_type | solution.py:64
  (16 shorter events, 0.1 us)
Async XLA Ops:
  7.2 7.0 %copy-start = (bf16[4096,256]{1,0:T(8,128)(2,1)S(1)}, bf16[4096,256]{1,0:T(8,128)(2,1)}, u32[]{:S(2)}) copy-start(bf16[4096,256]{1,0:T(8,128)(2,1)} %param.14) | copy-start | bytes 6291460
  7.2 4.5 %copy-start.10 = (bf16[4096]{0:T(1024)(128)(2,1)S(1)}, bf16[4096]{0:T(1024)(128)(2,1)}, u32[]{:S(2)}) copy-start(bf16[4096]{0:T(1024)(128)(2,1)} %param.11) | copy-start | bytes 24580
  7.2 4.5 %copy-start.11 = (bf16[4096]{0:T(1024)(128)(2,1)S(1)}, bf16[4096]{0:T(1024)(128)(2,1)}, u32[]{:S(2)}) copy-start(bf16[4096]{0:T(1024)(128)(2,1)} %param.12) | copy-start | bytes 24580
  7.2 119.1 %all-gather.3.cloned.1.call-start = ((), (), s32[]{:S(2)}) async-start(), calls=%async_computation.1 | async-start | bytes 9584640 | tf_op jit(solution)/shard_map/all_gather | solution.py:55
  7.3 4.5 %copy-start.2 = (bf16[256,4096]{1,0:T(8,128)(2,1)S(1)}, bf16[256,4096]{1,0:T(8,128)(2,1)}, u32[]{:S(2)}) copy-start(bf16[256,4096]{1,0:T(8,128)(2,1)} %param.10) | copy-start | bytes 6291460
  11.8 4.0 %copy-start.9 = (s32[256]{0:T(256)S(1)}, s32[256]{0:T(256)}, u32[]{:S(2)}) copy-start(s32[256]{0:T(256)} %param.19) | copy-start | bytes 3076
  12.8 1.3 copy-start.3
  15.1 5.5 %copy-start.4 = (bf16[256,4096]{1,0:T(8,128)(2,1)S(1)}, bf16[256,4096]{1,0:T(8,128)(2,1)}, u32[]{:S(2)}) copy-start(bf16[256,4096]{1,0:T(8,128)(2,1)} %copy-done.3) | copy-start | bytes 6291460
  29.0 3.6 %copy-start.8 = (pred[256,128]{1,0:T(8,128)(4,1)S(1)}, pred[256,128]{1,0:T(8,128)(4,1)}, u32[]{:S(2)}) copy-start(pred[256,128]{1,0:T(8,128)(4,1)} %broadcast_compare_fusion) | copy-start | bytes 98308
  30.2 15.2 %copy-start.6 = (bf16[256,2,32]{2,1,0:T(2,128)(2,1)}, bf16[256,2,32]{2,1,0:T(2,128)(2,1)S(1)}, u32[]{:S(2)}) copy-start(bf16[256,2,32]{2,1,0:T(2,128)(2,1)S(1)} %get-tuple-element.32) | copy-start | bytes 98308
  56.2 11.7 %copy-start.5 = (f32[256,2,4,1]{3,2,1,0:T(4,128)S(1)}, f32[256,2,4,1]{3,2,1,0:T(4,128)}, u32[]{:S(2)}) copy-start(f32[256,2,4,1]{3,2,1,0:T(4,128)} %copy.112) | copy-start | bytes 24580
  70.9 171.7 %all-reduce.2.cloned.1.call-start = ((), (), s32[]{:S(2)}) async-start(), calls=%async_computation | async-start | bytes 8388608 | tf_op jit(solution)/shard_map/psum | solution.py:63
  154.6 0.9 copy-start.7
  155.5 91.9 %copy-start.1 = (bf16[4096,256]{1,0:T(8,128)(2,1)S(1)}, bf16[4096,256]{1,0:T(8,128)(2,1)}, u32[]{:S(2)}) copy-start(bf16[4096,256]{1,0:T(8,128)(2,1)} %param.14) | copy-start | bytes 6291460
Sparse Core Ops, SparseCore 0:
  71.0 55.1 all-gather.2
  154.8 87.8 all-reduce.1
where the time goes:
time: 255 us; the launch traced here: 254 us
  waiting for transfers between devices  141 us (55%)
  matrix products  42.7 us (17%)
  other arithmetic  29.3 us (11%)
  local copies, waits for them, and re-layouts  26.4 us (10%)
  between operations  14.4 us (6%)
    psum x1, waiting for transfers between devices, local_step(): summed = lax.psum(partial_out, 'tp')  85.9 us
    all_gather x1, waiting for transfers between devices, local_step(): gathered = lax.all_gather(packed, 'sp', axis=0)  55.3 us
    dot_general x1, matrix products, local_step(): jnp.einsum('bkgd,bskd->bkgs', queries, k_cache, preferred_element_type=jn...  12.8 us
    dot_general x1, matrix products, local_step(): jnp.einsum('bkgs,bskd->bkgd', weights.astype(jnp.bfloat16), v_cache, pref...  11.7 us
    all_gather x1, local copies, waits for them, and re-layouts, local_step(): gathered = lax.all_gather(packed, 'sp', axis=0)  10.9 us
    dot_general x1, matrix products, local_step(): partial_out = jnp.dot(context, w_o, preferred_element_type=jnp.float32)  7.73 us
    reduce_sum x1, other arithmetic, local_step(): jnp.sum(gathered[..., :head_dim] * factor[..., None], axis=0)  6.68 us
    dot_general x1, matrix products, local_step(): jnp.dot(normed, w_q, preferred_element_type=jnp.float32)  5.7 us
  transfers between devices with their start and end apart: 2, of which 2 were waited for; matrix products, arithmetic and copies ran while one was open for 1% of the time, Pallas kernels for 0%

commit v1 on v0

v1 whole, which is shorter than its diff:
```python
import functools

import jax
import jax.numpy as jnp
from jax import lax
from jax.experimental import pallas as pl
from jax.experimental.pallas import tpu as pltpu
from jax.sharding import PartitionSpec as P

MESH = pl.DeviceIdType.MESH
F32 = jnp.float32
BF16 = jnp.bfloat16
NEG = float('-inf')
LANES = 128
RING = 4


def rotary_tables(lengths, head_dim):
    rot_dim = head_dim // 2
    half = rot_dim // 2
    inv_freq = 10000.0 ** (-2.0 * jnp.arange(half, dtype=F32) / rot_dim)
    angle = lengths.astype(F32)[:, None] * inv_freq
    cos, sin = jnp.cos(angle), jnp.sin(angle)
    rest = jnp.zeros((lengths.shape[0], head_dim - rot_dim), F32)
    return jnp.concatenate([cos, cos, rest + 1.0], axis=1), jnp.concatenate([-sin, sin, rest], axis=1)


def qkv_kernel(hid, gain, bias, cos, sin, wq, wk, wv, q_out, ks_out, vs_out, kn_out, vn_out, wbuf, normed, raw, pair, sem):
    rows, width = hid.shape
    q_cols, kv_cols = wq.shape[1], wk.shape[1]
    step = kv_cols
    kv_heads = kv_cols // LANES
    q_heads = q_cols // LANES
    group = q_heads // kv_heads
    q_steps = q_cols // step
    steps = q_steps + 2
    copies = [pltpu.make_async_copy(wq.at[:, pl.ds(j * step, step)], wbuf.at[j], sem.at[j]) for j in range(q_steps)]
    copies.append(pltpu.make_async_copy(wk, wbuf.at[q_steps], sem.at[q_steps]))
    copies.append(pltpu.make_async_copy(wv, wbuf.at[q_steps + 1], sem.at[q_steps + 1]))
    for c in copies:
        c.start()

    tile = 16
    scale_row = 1.0 + gain[...].astype(F32)
    bias_row = bias[...].astype(F32)

    def norm(i, _):
        r = pl.ds(pl.multiple_of(i * tile, tile), tile)
        wide = hid[r, :].astype(F32)
        centred = wide - jnp.sum(wide, axis=1, keepdims=True) * (1.0 / width)
        var = jnp.sum(centred * centred, axis=1, keepdims=True) * (1.0 / width)
        normed[r, :] = (centred * lax.rsqrt(var + 1e-5) * scale_row + bias_row).astype(BF16)
        return 0

    lax.fori_loop(0, rows // tile, norm, 0)

    lane = lax.broadcasted_iota(jnp.int32, (rows, LANES), 1)
    quarter = LANES // 4

    def rotate(u):
        swapped = jnp.where(lane < quarter, pltpu.roll(u, LANES - quarter, 1), pltpu.roll(u, quarter, 1))
        return u * cos[...] + swapped * sin[...]

    for j in range(steps):
        copies[j].wait()
        raw[...] = jnp.dot(normed[...], wbuf[j], preferred_element_type=F32)
        for i in range(kv_heads):
            u = raw[:, i * LANES:(i + 1) * LANES]
            if j < q_steps:
                h = j * kv_heads + i
                q_out[pl.ds(h, rows, stride=q_heads), :] = rotate(u).astype(BF16).astype(F32)
                continue
            if j == q_steps:
                u = rotate(u)
            u = u.astype(BF16).astype(F32)
            pair[pl.ds(i, rows, stride=kv_heads), :] = u
            spread = ks_out if j == q_steps else vs_out
            for g in range(group):
                spread[pl.ds(i * group + g, rows, stride=q_heads), :] = u
        if j == q_steps:
            kn_out[...] = pair[...].astype(BF16)
        if j == q_steps + 1:
            vn_out[...] = pair[...].astype(BF16)


def main_kernel(q, kself, vself, lens, k_hbm, v_hbm, wo_hbm, hid_hbm, out, kbuf, vbuf, wo, hid, part, from_core, relay, ctx32, ctx,
                prod, in_tp, full, kv_sem, wo_sem, hid_sem, d_send, d_recv, r_send, r_recv, u_send, u_recv, a_send, a_recv,
                b_send, b_recv, g_send, g_recv):
    dp, tp, sp = lax.axis_index('dp'), lax.axis_index('tp'), lax.axis_index('sp')
    core, x, y = sp % 2, sp // 2, tp
    blocks, rows = part.shape[0], hid.shape[0]
    heads = q.shape[0] // lens.shape[0]
    keys = kbuf.shape[1] // rows
    kv_local = 2
    seq = keys // kv_local
    group = heads // kv_local
    cols = hid.shape[1]
    stat = rows * heads
    turn = 1 - 2 * core

    def at(dx, dy, c):
        return {'dp': dp, 'tp': (y + dy + RING) % RING, 'sp': ((x + dx + RING) % RING) * 2 + c}

    def remote(src, dst, send, recv, to):
        return pltpu.make_async_remote_copy(src_ref=src, dst_ref=dst, send_sem=send, recv_sem=recv, device_id=to, device_id_type=MESH)

    partner = at(0, 0, 1 - core)
    neighbours = [partner, at(1, 0, core), at(-1, 0, core), at(0, 1, core), at(0, -1, core)]
    barrier = pltpu.get_barrier_semaphore()
    for to in neighbours:
        pl.semaphore_signal(barrier, inc=1, device_id=to, device_id_type=MESH)

    def order(c):
        t = 1 - 2 * c
        return [((x + d + RING) % RING) * 2 + c for d in (2, -t, t, 0)]

    mine, theirs = order(core), order(1 - core)
    sequence = [b for pair in zip(theirs, mine) for b in pair]
    kv_copies = []
    for i, b in enumerate(sequence):
        src = pl.ds(pl.multiple_of(b * rows * keys, rows * keys), rows * keys)
        kv_copies.append((pltpu.make_async_copy(k_hbm.at[src, :], kbuf.at[i], kv_sem.at[0, i]),
                          pltpu.make_async_copy(v_hbm.at[src, :], vbuf.at[i], kv_sem.at[1, i])))
        kv_copies[i][0].start()
        kv_copies[i][1].start()
    col_order = [(y + d + RING) % RING for d in (2, -turn, turn, 0)]
    wo_copies = [pltpu.make_async_copy(wo_hbm.at[:, pl.ds(pl.multiple_of(b * cols, cols), cols)], wo.at[i], wo_sem.at[i])
                 for i, b in enumerate(col_order)]
    for c in wo_copies:
        c.start()
    hid_copy = pltpu.make_async_copy(hid_hbm.at[pl.ds(pl.multiple_of(sp * rows, rows), rows), pl.ds(pl.multiple_of(tp * cols, cols), cols)],
                                     hid, hid_sem)
    hid_copy.start()

    key_id = lax.broadcasted_iota(jnp.int32, (heads, keys), 1)
    head_id = lax.broadcasted_iota(jnp.int32, (heads, keys), 0)
    position = jnp.where(key_id % kv_local == head_id // group, key_id // kv_local, 2 ** 30)
    lane = lax.broadcasted_iota(jnp.int32, (heads, LANES), 1)
    score_scale = LANES ** -0.5
    unroll = min(8, rows)

    def attend(i):
        b = sequence[i]
        for c in kv_copies[i]:
            c.wait()

        def some(it, carry):
            m_all, l_all = carry
            for u in range(unroll):
                r = it * unroll + u
                row = b * rows + r
                qh = pl.ds(pl.multiple_of(row * heads, heads), heads)
                kh = pl.ds(pl.multiple_of(r * keys, keys), keys)
                query = q[qh, :]
                s = lax.dot_general(query.astype(BF16), kbuf[i, kh, :], (((1,), (1,)), ((), ())), preferred_element_type=F32) * score_scale
                n = lens[row] - sp * seq
                s = jnp.where(position < n, s, NEG)
                owner = jnp.where(jnp.logical_and(n >= 0, n < seq), 0.0, NEG)
                s_self = jnp.sum(query * kself[qh, :], axis=1, keepdims=True) * score_scale + owner
                m = jnp.maximum(jnp.max(s, axis=1, keepdims=True), s_self)
                safe = jnp.where(m == NEG, 0.0, m)
                w = jnp.exp(s - safe)
                w_self = jnp.exp(s_self - safe)
                total = jnp.sum(w, axis=1, keepdims=True) + w_self
                o = jnp.dot(w.astype(BF16), vbuf[i, kh, :], preferred_element_type=F32) + w_self * vself[qh, :]
                part[i, pl.ds(pl.multiple_of(r * heads, heads), heads), :] = o
                m_all = jnp.where(lane == r, m, m_all)
                l_all = jnp.where(lane == r, total, l_all)
            return m_all, l_all

        m_all, l_all = lax.fori_loop(0, rows // unroll, some, (jnp.zeros((heads, LANES), F32), jnp.ones((heads, LANES), F32)))
        part[i, stat:stat + heads, :] = m_all
        part[i, stat + heads:stat + 2 * heads, :] = l_all

    def combine(sources, last=False):
        ms = [s[stat:stat + heads, :] for s in sources]
        top = functools.reduce(jnp.maximum, ms)
        safe = jnp.where(top == NEG, 0.0, top)
        fs = [jnp.exp(m - safe) for m in ms]
        total = functools.reduce(jnp.add, [f * s[stat + heads:stat + 2 * heads, :] for f, s in zip(fs, sources)])
        if last:
            fs = [f / total for f in fs]
        for r in range(rows):
            span = slice(r * heads, (r + 1) * heads)
            acc = functools.reduce(jnp.add, [s[span, :] * f[:, r:r + 1] for f, s in zip(fs, sources)])
            if last:
                ctx32[span, :] = acc
            else:
                sources[0][span, :] = acc
        if not last:
            sources[0][stat:stat + heads, :] = top
            sources[0][stat + heads:stat + 2 * heads, :] = total

    with_turn, against = at(turn, 0, core), at(-turn, 0, core)
    cross = [remote(part.at[2 * k], from_core.at[k], d_send.at[k], d_recv.at[k], partner) for k in range(4)]
    hops = [remote(part.at[1], relay.at[0], r_send.at[0], r_recv.at[0], with_turn),
            remote(part.at[3], relay.at[2], r_send.at[2], r_recv.at[2], against),
            remote(part.at[5], relay.at[1], r_send.at[1], r_recv.at[1], with_turn)]
    for k in range(4):
        attend(2 * k)
        if k == 0:
            pl.semaphore_wait(barrier, len(neighbours))
        cross[k].start()
        attend(2 * k + 1)
        cross[k].wait_recv()
        sources = [part.at[2 * k + 1], from_core.at[k]]
        if k == 2:
            hops[0].wait_recv()
            sources.append(relay.at[0])
        if k == 3:
            hops[2].wait_recv()
            hops[1].wait_recv()
            sources += [relay.at[1], relay.at[2]]
        combine(sources, last=k == 3)
        if k < 3:
            hops[k].start()

    for h in range(heads):
        ctx[:, h * LANES:(h + 1) * LANES] = ctx32[pl.ds(h, rows, stride=heads), :].astype(BF16)

    up, down = at(0, turn, core), at(0, -turn, core)
    halves = 2
    half = rows // halves
    lands = [0, 2, 1]
    out_tp = []
    for k in range(3):
        pieces = []
        for p in range(halves):
            span = pl.ds(p * half, half)
            pieces.append(remote(prod.at[k, span, :], in_tp.at[lands[k], span, :], u_send.at[lands[k], p], u_recv.at[lands[k], p],
                                 down if k == 1 else up))
        out_tp.append(pieces)
    tile = min(cols, 512)
    for k in range(4):
        wo_copies[k].wait()
        for t in range(0, cols, tile):
            prod[k, :, t:t + tile] = jnp.dot(ctx[...], wo[k, :, t:t + tile], preferred_element_type=F32)
        if k < 2:
            for piece in out_tp[k]:
                piece.start()
    for p in range(halves):
        span = pl.ds(p * half, half)
        out_tp[0][p].wait_recv()
        prod[2, span, :] = prod[2, span, :] + in_tp[0, span, :]
        out_tp[2][p].start()
    hid_copy.wait()
    for p in range(halves):
        span = pl.ds(p * half, half)
        out_tp[1][p].wait_recv()
        out_tp[2][p].wait_recv()
        full[sp, tp, span, :] = hid[span, :].astype(F32) + (prod[3, span, :] + in_tp[2, span, :] + in_tp[1, span, :])

    offset = (0, -1, 1, 2)

    def place(c, k1, k2):
        o1, o2 = offset[k1], offset[k2]
        cx = (x + o1 * (1 - c) + o2 * c + RING) % RING
        cy = (y + o1 * c + o2 * (1 - c) + RING) % RING
        return cx * 2 + c, cy

    def chunk(c, k1, k2, piece=None):
        s, t = place(c, k1, k2)
        if piece is None:
            return full.at[s, t]
        return full.at[s, t, pl.ds(piece * half, half), :]

    def narrow(c, k1, k2):
        s, t = place(c, k1, k2)
        out[pl.ds(pl.multiple_of(s * rows, rows), rows), pl.ds(pl.multiple_of(t * cols, cols), cols)] = full[s, t].astype(BF16)

    first = [at(1 - core, core, core), at(core - 1, -core, core)]
    second = [at(core, 1 - core, core), at(-core, core - 1, core)]
    started = []

    def go(copy):
        copy.start()
        started.append(copy)

    def arrived(view, recv):
        remote(view, view, recv, recv, partner).wait_recv()

    def spread(k1):
        for d in range(2):
            go(remote(chunk(core, k1, 0), chunk(core, k1, 0), b_send.at[k1, d], b_recv.at[k1, d], second[d]))
        share(k1, 0)

    def share(k1, k2):
        go(remote(chunk(core, k1, k2), chunk(core, k1, k2), g_send.at[k1, k2], g_recv.at[k1, k2], partner))
        narrow(core, k1, k2)

    def along(k1):
        for d in range(2):
            arrived(chunk(core, k1, 1 + d), b_recv.at[k1, d])
            go(remote(chunk(core, k1, 1 + d, d), chunk(core, k1, 1 + d, d), b_send.at[k1, 2 + d], b_recv.at[k1, 2 + d], second[d]))
            share(k1, 1 + d)

    def far(k1):
        for d in range(2):
            arrived(chunk(core, k1, 3, d), b_recv.at[k1, 2 + d])
        share(k1, 3)

    for d in range(2):
        go(remote(chunk(core, 0, 0), chunk(core, 0, 0), a_send.at[d], a_recv.at[d], first[d]))
    spread(0)
    for d in range(2):
        arrived(chunk(core, 1 + d, 0), a_recv.at[d])
        go(remote(chunk(core, 1 + d, 0, d), chunk(core, 1 + d, 0, d), a_send.at[2 + d], a_recv.at[2 + d], first[d]))
        spread(1 + d)
    along(0)
    for d in range(2):
        arrived(chunk(core, 3, 0, d), a_recv.at[2 + d])
    spread(3)
    along(1)
    along(2)
    far(0)
    along(3)
    far(1)
    far(2)
    far(3)
    turns = [(0, 0), (1, 0), (2, 0), (0, 1), (0, 2), (3, 0), (1, 1), (1, 2), (2, 1), (2, 2), (0, 3), (3, 1), (3, 2), (1, 3), (2, 3), (3, 3)]
    for k1, k2 in turns:
        arrived(chunk(1 - core, k1, k2), g_recv.at[k1, k2])
        narrow(1 - core, k1, k2)
    for copy in cross + hops + [p for pieces in out_tp for p in pieces] + started:
        copy.wait_send()


def solution(mesh):
    tp_size, sp_size = mesh.shape['tp'], mesh.shape['sp']
    assert tp_size == RING and sp_size == 2 * RING

    def local_step(hidden, ln_gain, ln_bias, w_q, w_k, w_v, w_o, k_cache, v_cache, lengths):
        batch, seq_local, kv_local, head_dim = k_cache.shape
        assert head_dim == LANES and kv_local == 2
        width = hidden.shape[1]
        heads = w_q.shape[1] // head_dim
        step = w_k.shape[1]
        steps = w_q.shape[1] // step + 2
        rows, cols = batch // sp_size, w_o.shape[1] // tp_size
        keys = seq_local * kv_local
        cos, sin = rotary_tables(lengths, head_dim)
        vmem = pl.BlockSpec(memory_space=pltpu.VMEM)
        hbm = pl.BlockSpec(memory_space=pl.ANY)
        smem = pl.BlockSpec(memory_space=pltpu.SMEM)
        flat = jax.ShapeDtypeStruct((batch * heads, head_dim), F32)
        new = jax.ShapeDtypeStruct((batch * kv_local, head_dim), BF16)
        q, kself, vself, k_new, v_new = pl.pallas_call(
            qkv_kernel,
            out_shape=(flat, flat, flat, new, new),
            in_specs=[vmem] * 5 + [hbm] * 3,
            out_specs=(vmem,) * 5,
            scratch_shapes=[
                pltpu.VMEM((steps, width, step), BF16),
                pltpu.VMEM((batch, width), BF16),
                pltpu.VMEM((batch, step), F32),
                pltpu.VMEM((batch * kv_local, head_dim), F32),
                pltpu.SemaphoreType.DMA((steps,)),
            ],
            compiler_params=pltpu.CompilerParams(vmem_limit_bytes=40 * 2 ** 20),
            name='qkv',
        )(hidden, ln_gain.reshape(1, -1), ln_bias.reshape(1, -1), cos, sin, w_q, w_k, w_v)
        blocks = sp_size
        slab = rows * heads + 2 * heads
        dma = pltpu.SemaphoreType.DMA
        out = pl.pallas_call(
            main_kernel,
            out_shape=jax.ShapeDtypeStruct((batch, w_o.shape[1]), BF16),
            in_specs=[vmem] * 3 + [smem] + [hbm] * 4,
            out_specs=vmem,
            scratch_shapes=[
                pltpu.VMEM((blocks, rows * keys, head_dim), BF16),
                pltpu.VMEM((blocks, rows * keys, head_dim), BF16),
                pltpu.VMEM((tp_size, w_o.shape[0], cols), BF16),
                pltpu.VMEM((rows, cols), BF16),
                pltpu.VMEM((blocks, slab, head_dim), F32),
                pltpu.VMEM((4, slab, head_dim), F32),
                pltpu.VMEM((3, slab, head_dim), F32),
                pltpu.VMEM((rows * heads, head_dim), F32),
                pltpu.VMEM((rows, w_o.shape[0]), BF16),
                pltpu.VMEM((4, rows, cols), F32),
                pltpu.VMEM((3, rows, cols), F32),
                pltpu.VMEM((sp_size, tp_size, rows, cols), F32),
                dma((2, blocks)), dma((4,)), dma,
                dma((4,)), dma((4,)), dma((3,)), dma((3,)), dma((3, 2)), dma((3, 2)),
                dma((4,)), dma((4,)), dma((4, 4)), dma((4, 4)), dma((4, 4)), dma((4, 4)),
            ],
            compiler_params=pltpu.CompilerParams(vmem_limit_bytes=62 * 2 ** 20, collective_id=0, has_side_effects=True),
            name='attend_sum_gather',
        )(q, kself, vself, lengths, k_cache.reshape(-1, head_dim), v_cache.reshape(-1, head_dim), w_o, hidden)
        shape = (batch, kv_local, head_dim)
        return out, k_new.reshape(shape), v_new.reshape(shape)

    row_spec = P('dp', None)
    cache_spec = P('dp', 'sp', 'tp', None)
    head_spec = P('dp', 'tp', None)
    return jax.shard_map(local_step, mesh=mesh, in_specs=(row_spec, P(None), P(None), P(None, 'tp'), P(None, 'tp'), P(None, 'tp'), P('tp', None), cache_spec, cache_spec, P('dp')), out_specs=(row_spec, head_spec, head_spec), check_vma=False)
```

time: 255 us -> 134 us (0.53)
  waiting for transfers between devices: 141 us -> 0 us
  Pallas kernels: 0 us -> 119 us
  matrix products: 42.7 us -> 0 us
  other arithmetic: 29.3 us -> 1.37 us
  local copies, waits for them, and re-layouts: 26.4 us -> 12.4 us
  between operations: 14.4 us -> 0.69 us
    pallas_call x0 -> x2, Pallas kernels: none -> 119 us  [the longest x1 105 us: local_step(): pl.pallas_call(main_kernel, out_shape=jax.ShapeDtypeStruct((batch, w_o.sh...]
    psum x1 -> x0, waiting for transfers between devices: 85.9 us -> none  [local_step(): summed = lax.psum(partial_out, 'tp')]
    all_gather x1 -> x0, waiting for transfers between devices: 55.3 us -> none  [local_step(): gathered = lax.all_gather(packed, 'sp', axis=0)]
    dot_general x7 -> x0, matrix products: 42.7 us -> none  [the longest x1 12.8 us: local_step(): jnp.einsum('bkgd,bskd->bkgs', queries, k_cache, preferred_element_type=jn...]
    reduce_sum x5 -> x0, other arithmetic: 13.4 us -> none  [the longest x1 6.68 us: local_step(): jnp.sum(gathered[..., :head_dim] * factor[..., None], axis=0)]
    all_gather x1 -> x0, local copies, waits for them, and re-layouts: 10.9 us -> none  [local_step(): gathered = lax.all_gather(packed, 'sp', axis=0)]
    unnamed x28 -> x13, local copies, waits for them, and re-layouts: 3.46 us -> 10.8 us
    broadcast_in_dim x2 -> x1, local copies, waits for them, and re-layouts: 7.29 us -> 0.01 us  [rotary_tables(): rest = jnp.zeros((lengths.shape[0], head_dim - rot_dim), F32)]
  transfers between devices with their start and end apart: 2 -> 0, of which waited for: 2 -> 0; matrix products, arithmetic and copies ran while one was open for 1% -> 0% of each run, Pallas kernels for 0% -> 0%
where the time goes in v1:
time: 134 us; the launch traced here: 133 us
  Pallas kernels  119 us (89%)
  local copies, waits for them, and re-layouts  12.4 us (9%)
  other arithmetic  1.37 us (1%)
    pallas_call x1, Pallas kernels, local_step(): pl.pallas_call(main_kernel, out_shape=jax.ShapeDtypeStruct((batch, w_o.sh...  105 us
    pallas_call x1, Pallas kernels, local_step(): pl.pallas_call(qkv_kernel, out_shape=(flat, flat, flat, new, new), in_spe...  13.6 us
    unnamed x13, local copies, waits for them, and re-layouts  10.8 us

profile of v1, /device:TPU:97, one launch (start us, length us, event | category | flops | bytes accessed | tf_op | source)
XLA Modules:
  0.0 133.2 jit_solution(16170428632775351582)
XLA Ops:
  0.6 0.1 pad.5.clone
  0.7 0.1 pad.2.clone
  0.8 0.7 convert_element_type.3
  1.5 0.7 reshape.30.gain
  2.2 0.7 reshape.31.bias
  2.9 0.5 fusion
  3.5 0.1 maximum_maximum_fusion
  3.6 0.0 copy-start
  3.6 1.6 %copy-done = bf16[256,4096]{1,0:T(8,128)(2,1)S(1)} copy-done((bf16[256,4096]{1,0:T(8,128)(2,1)S(1)}, bf16[256,4096]{1,0:T(8,128)(2,1)}, u32[]{:S(2)}) %copy-start) | copy-done | bytes 2097176
  5.2 0.0 copy-start.1
  5.2 1.6 %copy-done.1 = bf16[4096,256]{1,0:T(8,128)(2,1)S(1)} copy-done((bf16[4096,256]{1,0:T(8,128)(2,1)S(1)}, bf16[4096,256]{1,0:T(8,128)(2,1)}, u32[]{:S(2)}) %copy-start.1) | copy-done | bytes 2097176
  6.8 0.0 copy-start.2
  6.8 1.6 %copy-done.2 = bf16[4096,256]{1,0:T(8,128)(2,1)S(1)} copy-done((bf16[4096,256]{1,0:T(8,128)(2,1)S(1)}, bf16[4096,256]{1,0:T(8,128)(2,1)}, u32[]{:S(2)}) %copy-start.2) | copy-done | bytes 2097176
  8.4 13.6 %qkv.1 = (f32[2048,128]{1,0:T(8,128)S(1)}, f32[2048,128]{1,0:T(8,128)S(1)}, f32[2048,128]{1,0:T(8,128)S(1)}, bf16[512,128]{1,0:T(8,128)(2,1)}, bf16[512,128]{1,0:T(8,128)(2,1)}) custom-call(bf16[256,4096]{1,0:T(8,128)(2,1)S(1)} %copy-done, bf16[1,4096]{1,0:T(2,128)(2,1)S(1)} %reshape.30.gain, bf16[1,4096]{1,0:T(2,128)(2,1)S(1)} %reshape.31.bias, ...), custom_call_target="tpu_custom_call" | custom-call | tf_op jit(solution)/shard_map/qkv/pallas_call | solution.py:347
  22.0 0.0 copy-start.3
  22.0 1.0 copy-done.3
  23.0 0.0 copy-start.4
  23.0 1.0 copy-done.4
  24.0 0.0 copy-start.5
  24.0 1.0 copy-done.5
  24.9 105.1 %attend_sum_gather.1 = bf16[256,4096]{1,0:T(8,128)(2,1)} custom-call(f32[2048,128]{1,0:T(8,128)} %copy-done.3, f32[2048,128]{1,0:T(8,128)} %copy-done.4, f32[2048,128]{1,0:T(8,128)} %copy-done.5, s32[256]{0:T(256)} %lens.1, bf16[65536,128]{1,0:T(8,128)(2,1)} %bitcast.4, bf16[65536,128]{1,0:T(8,128)(2,1)} %bitcast.5, bf16[1024,4096]{1,0:T(8,128)(2,1)} %wo_hbm.1, ...), custom_call_target="tpu_custom_call" | custom-call | tf_op jit(solution)/shard_map/attend_sum_gather/pallas_call | solution.py:365
  130.1 3.1 %copy.15 = bf16[256,4096]{1,0:T(8,128)(2,1)} copy(bf16[256,4096]{1,0:T(8,128)(2,1)} %attend_sum_gather.1) | data formatting | bytes 4194304
  (3 shorter events, 0.0 us)
Async XLA Ops:
  3.6 1.6 %copy-start = (bf16[256,4096]{1,0:T(8,128)(2,1)S(1)}, bf16[256,4096]{1,0:T(8,128)(2,1)}, u32[]{:S(2)}) copy-start(bf16[256,4096]{1,0:T(8,128)(2,1)} %hid_hbm.1) | copy-start | bytes 6291460
  5.2 1.6 %copy-start.1 = (bf16[4096,256]{1,0:T(8,128)(2,1)S(1)}, bf16[4096,256]{1,0:T(8,128)(2,1)}, u32[]{:S(2)}) copy-start(bf16[4096,256]{1,0:T(8,128)(2,1)} %wk.1) | copy-start | bytes 6291460
  6.8 1.6 %copy-start.2 = (bf16[4096,256]{1,0:T(8,128)(2,1)S(1)}, bf16[4096,256]{1,0:T(8,128)(2,1)}, u32[]{:S(2)}) copy-start(bf16[4096,256]{1,0:T(8,128)(2,1)} %wv.1) | copy-start | bytes 6291460
  22.0 1.0 copy-start.3
  23.0 1.0 copy-start.4
  24.0 1.0 copy-start.5
